TPU v7x, 256 devices: a whole 4x4x8 slice. The times are simulated.
256 devices in a mesh: row: 16 (over z, core), col: 16 (over y, x).
Axes of the slice: x: 4, y: 4, z: 8, core: 2. Of those that a mesh axis runs over, the one named last changes fastest.
Arguments:
- act_codes: int32 [2048, 7168], P('col', 'row'), may hold values from -127 to 127
- act_scales: float32 [2048, 112], P('col', 'row'), may hold values from 0.005 to 0.03
- gate_weight: bfloat16 [7168, 18432], P('row', 'col'), may hold values from -0.0625 to 0.0625
- up_weight: bfloat16 [7168, 18432], P('row', 'col'), may hold values from -0.0625 to 0.0625
- down_weight: bfloat16 [18432, 7168], P('col', 'row'), may hold values from -0.046875 to 0.046875
Outputs:
- mixed: bfloat16 [2048, 7168], P('col', 'row')
All inputs are finite; a program needn't handle non-finite values.
Results may differ from a plain program's by a relative error of at most 0.03.
Values may be sent and summed in bfloat16 or wider, within the bound.
A program may use at most 128 MiB of HBM per device.

v0:
```python
import jax
import jax.numpy as jnp
from jax import lax
from jax.sharding import Mesh
from jax.sharding import PartitionSpec as P

ROW = ("row_0", "row_1")


def in_order(tiles, dim):
    tiles = jnp.moveaxis(tiles, 0, dim)
    lengths = tiles.shape
    return tiles.reshape(*lengths[:dim], lengths[dim] * lengths[dim + 1], *lengths[dim + 2 :])


def sent_to_all(array, axis):
    copies = jnp.broadcast_to(array, (lax.axis_size(axis), *array.shape))
    return lax.all_to_all(copies, axis, split_axis=0, concat_axis=0, tiled=True)


def gather_directly(array, axis, dim):
    return in_order(sent_to_all(array, axis), dim)


def own_block(tiles, axes, order):
    lengths = [lax.axis_size(a) for a in axes]
    tiles = tiles.reshape(*lengths, *tiles.shape[1:])
    tiles = tiles.transpose(*order, *range(len(axes), tiles.ndim))
    tiles = tiles.reshape(-1, *tiles.shape[len(axes) :])
    for k in order:
        tiles = lax.psum_scatter(tiles, axes[k], scatter_dimension=0, tiled=True)
    return tiles[0]


def cut_along(array, dim, length):
    before, after = (array.shape[:dim], array.shape[dim + 1 :])
    return jnp.moveaxis(array.reshape(*before, length, -1, *after), dim, 0)


def scatter_axes(array, axes, order, dim):
    length = lax.axis_size(axes)
    return own_block(cut_along(array, dim, length), axes, order)


def sent_and_summed(array, axis, dim):
    length = lax.axis_size(axis)
    tiles = lax.all_to_all(cut_along(array, dim, length), axis, 0, 0, tiled=True)
    return jnp.sum(tiles.astype(jnp.float32), axis=0)


def on_device(act_codes, act_scales, gate_weight, up_weight, down_weight):
    local_rows = act_codes.shape[0]
    width = act_codes.shape[1]
    nblocks = act_scales.shape[1]
    blocked = act_codes.astype(jnp.float32).reshape(local_rows, nblocks, width // nblocks)
    acts = (blocked * act_scales[:, :, None]).reshape(local_rows, width).astype(jnp.bfloat16)
    every = gather_directly(acts, "col", 0)
    hidden_width = gate_weight.shape[1]
    gate_part = jnp.dot(every, gate_weight, preferred_element_type=jnp.float32)
    up_part = jnp.dot(every, up_weight, preferred_element_type=jnp.float32)
    summed = scatter_axes(
        jnp.concatenate([gate_part, up_part], axis=1).astype(jnp.bfloat16), ROW, (1, 0), 0
    ).astype(jnp.float32)
    hidden = (jax.nn.silu(summed[:, :hidden_width]) * summed[:, hidden_width:]).astype(jnp.bfloat16)
    partial_value = jnp.dot(
        lax.all_gather(hidden, ROW, axis=0, tiled=True),
        down_weight,
        preferred_element_type=jnp.float32,
    )
    mixed = sent_and_summed(partial_value.astype(jnp.bfloat16), "col", 0)
    return mixed.astype(jnp.bfloat16)


def solution(mesh):
    torus = Mesh(mesh.devices.reshape(8, 2, mesh.shape["col"]), ("row_0", "row_1", "col"))
    in_specs = (P("col", ROW), P("col", ROW), P(ROW, "col"), P(ROW, "col"), P("col", ROW))
    out_specs = P("col", ROW)
    return jax.shard_map(
        on_device, mesh=torus, in_specs=in_specs, out_specs=out_specs, check_vma=False
    )
```

profile of v0, /device:TPU:1, one launch (start us, length us, event | category | flops | bytes accessed | tf_op | source)
XLA Modules:
  0.0 233.5 jit_solution(17031267609659101783)
XLA Ops:
  6.5 0.0 copy-start
  6.5 0.0 reduce-scatter.3.cloned.1.call-start
  6.5 1.1 fusion.4
  7.6 0.3 broadcast_in_dim.4
  8.0 32.1 %all_to_all.10 = bf16[16,128,448]{1,2,0:T(8,128)(2,1)S(1)} all-to-all(bf16[16,128,448]{1,2,0:T(8,128)(2,1)S(1)} %broadcast_in_dim.4), channel_id=1, replica_groups=mesh['row_0'=8,'row_1'=2,'col'=16] {'col'}, dimensions={0} | all-to-all | bytes 3670016 | tf_op jit(solution)/shard_map/all_to_all | solution.py:18
  40.1 0.0 copy-start.1
  40.1 0.0 copy-done
  40.1 3.2 %convolution_convert_fusion = bf16[8,2,128,1152]{3,2,1,0:T(8,128)(2,1)S(1)} fusion(bf16[8,2,128,448]{2,3,1,0:T(8,128)(2,1)S(1)} %bitcast.32, bf16[448,1152]{1,0:T(8,128)(2,1)S(1)} %copy-done), kind=kOutput, calls=%fused_computation.1 | convolution fusion | flops 2116288512 | bytes 7585792 | tf_op jit(solution)/shard_map/dot_general | solution.py:60
  43.3 0.0 copy-done.1
  43.3 3.2 %convolution_convert_fusion.1 = bf16[8,2,128,1152]{3,2,1,0:T(8,128)(2,1)S(1)} fusion(bf16[8,2,128,448]{2,3,1,0:T(8,128)(2,1)S(1)} %bitcast.33, bf16[448,1152]{1,0:T(8,128)(2,1)S(1)} %copy-done.1), kind=kOutput, calls=%fused_computation.2 | convolution fusion | flops 2116288512 | bytes 7585792 | tf_op jit(solution)/shard_map/dot_general | solution.py:59
  46.4 4.0 %maximum_bitcast_fusion = bf16[2,8,128,2304]{3,2,0,1:T(8,128)(2,1)} fusion(bf16[8,2,128,1152]{3,2,1,0:T(8,128)(2,1)S(1)} %convolution_convert_fusion, bf16[8,2,128,1152]{3,2,1,0:T(8,128)(2,1)S(1)} %convolution_convert_fusion.1), kind=kLoop, calls=%fused_computation | loop fusion | flops 18874368 | bytes 18874368 | tf_op jit(solution)/shard_map/transpose | solution.py:28
  50.5 8.1 %copy.7 = bf16[2,8,128,2304]{3,2,1,0:T(8,128)(2,1)} copy(bf16[2,8,128,2304]{3,2,0,1:T(8,128)(2,1)} %maximum_bitcast_fusion) | data formatting | bytes 18874368 | tf_op jit(solution)/shard_map/transpose | solution.py:28
  58.6 0.0 reduce-scatter.3.cloned.1.call-update
  58.6 0.0 copy-start.2
  58.6 0.0 reduce-scatter.5.cloned.1.call-start
  58.7 23.4 %reduce-scatter.3.cloned.1.call-done = bf16[8,128,2304]{2,1,0:T(8,128)(2,1)} async-done(((bf16[16,128,2304]{2,1,0:T(8,128)(2,1)}), bf16[8,128,2304]{2,1,0:T(8,128)(2,1)}) %reduce-scatter.3.cloned.1.call-update) | async-done | bytes 4718608 | tf_op jit(solution)/shard_map/reduce_scatter | solution.py:31
  82.1 0.0 reduce-scatter.5.cloned.1.call-update
  82.1 0.0 all-gather.2.cloned.1.call-start
  82.1 63.5 %reduce-scatter.5.cloned.1.call-done = bf16[1,128,2304]{2,1,0:T(8,128)(2,1)} async-done(((bf16[8,128,2304]{2,1,0:T(8,128)(2,1)}), bf16[1,128,2304]{2,1,0:T(8,128)(2,1)}) %reduce-scatter.5.cloned.1.call-update) | async-done | bytes 589840 | tf_op jit(solution)/shard_map/reduce_scatter | solution.py:31
  145.7 1.1 bitcast_convert_fusion
  146.8 0.9 fusion.3
  147.7 0.0 all-gather.2.cloned.1.call-update
  147.7 41.5 %all-gather.2.cloned.1.call-done = bf16[2048,1152]{1,0:T(8,128)(2,1)} async-done(((bf16[128,1152]{1,0:T(8,128)(2,1)}), bf16[2048,1152]{1,0:T(8,128)(2,1)}) %all-gather.2.cloned.1.call-update) | async-done | bytes 4718608 | tf_op jit(solution)/shard_map/all_gather | solution.py:66
  189.2 0.0 copy-done.2
  189.2 4.9 %fusion = bf16[56,16,8,128]{3,2,1,0:T(8,128)(2,1)S(1)} fusion(bf16[2048,1152]{1,0:T(8,128)(2,1)} %all-gather.2.cloned.1.call-done, bf16[1152,448]{0,1:T(8,128)(2,1)S(1)} %copy-done.2), kind=kOutput, calls=%fused_computation.5 | convolution fusion | flops 2114846720 | bytes 7585792 | tf_op jit(solution)/shard_map/dot_general | solution.py:65
  194.1 0.5 copy.13
  194.6 31.5 %all_to_all.11 = bf16[16,128,448]{1,2,0:T(8,128)(2,1)S(1)} all-to-all(bf16[16,128,448]{1,2,0:T(8,128)(2,1)S(1)} %bitcast.31), channel_id=1, replica_groups=mesh['row_0'=8,'row_1'=2,'col'=16] {'col'}, dimensions={0} | all-to-all | bytes 3670016 | tf_op jit(solution)/shard_map/all_to_all | solution.py:47
  226.1 0.9 reduce_sum.12
Async XLA Ops:
  6.5 33.6 %copy-start = (bf16[448,1152]{1,0:T(8,128)(2,1)S(1)}, bf16[448,1152]{1,0:T(8,128)(2,1)}, u32[]{:S(2)}) copy-start(bf16[448,1152]{1,0:T(8,128)(2,1)} %param.8) | copy-start | bytes 3096580
  6.5 75.5 %reduce-scatter.3.cloned.1.call-start = ((), (), s32[]{:S(2)}) async-start(), calls=%async_computation.4 | async-start | bytes 14155776 | tf_op jit(solution)/shard_map/reduce_scatter | solution.py:31
  40.1 3.2 %copy-start.1 = (bf16[448,1152]{1,0:T(8,128)(2,1)S(1)}, bf16[448,1152]{1,0:T(8,128)(2,1)}, u32[]{:S(2)}) copy-start(bf16[448,1152]{1,0:T(8,128)(2,1)} %param.7) | copy-start | bytes 3096580
  58.6 130.6 %copy-start.2 = (bf16[1152,448]{0,1:T(8,128)(2,1)S(1)}, bf16[1152,448]{0,1:T(8,128)(2,1)}, u32[]{:S(2)}) copy-start(bf16[1152,448]{0,1:T(8,128)(2,1)} %param.9) | copy-start | bytes 3096580
  58.6 87.0 %reduce-scatter.5.cloned.1.call-start = ((), (), s32[]{:S(2)}) async-start(), calls=%async_computation.5 | async-start | bytes 5308416 | tf_op jit(solution)/shard_map/reduce_scatter | solution.py:31
  82.1 107.1 %all-gather.2.cloned.1.call-start = ((), (), s32[]{:S(2)}) async-start(), calls=%async_computation.6 | async-start | bytes 5013504 | tf_op jit(solution)/shard_map/all_gather | solution.py:66
Sparse Core Ops, SparseCore 0:
  58.7 23.2 reduce-scatter.2
  84.6 60.9 reduce-scatter.4
  147.9 41.2 all-gather.1
where the time goes:
time: 234 us; the launch traced here: 233 us
  waiting for transfers between devices  128 us (55%)
  blocking collectives  63.6 us (27%)
  between operations  13.2 us (6%)
  matrix products  11.2 us (5%)
  local copies, waits for them, and re-layouts  8.97 us (4%)
  other arithmetic  8.02 us (3%)
    reduce_scatter x2, waiting for transfers between devices, own_block(): tiles = lax.psum_scatter(tiles, axes[k], scatter_dimension=0, tiled=True)  86.9 us
    all_gather x1, waiting for transfers between devices, on_device(): lax.all_gather(hidden, ROW, axis=0, tiled=True)  41.5 us
    all_to_all x1, blocking collectives, sent_to_all(): return lax.all_to_all(copies, axis, split_axis=0, concat_axis=0, tiled=True)  32.1 us
    all_to_all x1, blocking collectives, sent_and_summed(): lax.all_to_all(cut_along(array, dim, length), axis, 0, 0, tiled=True)  31.5 us
    transpose x1, local copies, waits for them, and re-layouts, own_block(): tiles = tiles.transpose(*order, *range(len(axes), tiles.ndim))  8.14 us
    dot_general x1, matrix products, on_device(): jnp.dot(lax.all_gather(hidden, ROW, axis=0, tiled=True), down_weight, pre...  4.9 us
  transfers between devices with their start and end apart: 3, of which 3 were waited for; matrix products, arithmetic and copies ran while one was open for 0% of the time, Pallas kernels for 0%

commit v1 on v0

v1 whole, which is shorter than its diff:
```python
import functools

import jax
import jax.numpy as jnp
from jax import lax
from jax.experimental import pallas as pl
from jax.experimental.pallas import tpu as pltpu
from jax.sharding import PartitionSpec as P

MESH = pl.DeviceIdType.MESH
F32 = jnp.float32
BF16 = jnp.bfloat16

NZ, NX, NY, CORES = 8, 4, 4, 2
TOK = 128
HALF = TOK // CORES
D_ROW = 448
LOW = 384
D_CHIP = CORES * D_ROW
FF = 1152
GU = 2 * FF
PAD = 512
PIECE = 32
STRIP = 16
QB = 64

GROUPS = (
    ((0, 0), (1, 0), (3, 0), (0, 1)),
    ((0, 3), (1, 1), (2, 0), (0, 2)),
    ((1, 3), (3, 1), (3, 3), (1, 2)),
    ((3, 2), (2, 1), (2, 3), (2, 2)),
)
NQ = len(GROUPS)
SLOT = {s: i for i, s in enumerate(s for g in GROUPS for s in g)}
ROWS = HALF * 4
PASS_ON = {
    (0, 0): ((1, 0), (-1, 0), (0, 1), (0, -1)),
    (1, 0): ((0, 1), (0, -1), (1, 0)),
    (3, 0): ((0, 1), (0, -1)),
    (0, 1): ((0, 1),),
    (1, 1): ((0, 1),),
    (3, 3): ((0, -1),),
    (2, 0): ((0, 1), (0, -1)),
    (2, 3): ((0, -1),),
}
LAST = NZ - 1
HOPS = NZ // 2


def steps_of(part, slot):
    if part == 0:
        return PASS_ON.get(slot, ())
    return tuple((b, a) for a, b in PASS_ON.get((slot[1], slot[0]), ()))


def max_hop(d, q):
    return HOPS if (q + d) % 2 == 0 else HOPS - 1


def order():
    hops = {1: [(1, 0), (3, 0), (0, 1), (0, 3)],
            2: [(2, 0), (0, 2), (1, 1), (3, 1), (1, 3), (3, 3)],
            3: [(1, 2), (2, 1), (3, 2), (2, 3)],
            4: [(2, 2)]}
    ops = []
    for tick in range(LAST + HOPS + NQ):
        if tick < NQ:
            ops += [("acts", s) for s in hops[tick + 1]]
            ops += [("up", tick)]
        for q in reversed(range(NQ)):
            stage = tick - q
            if 0 <= stage <= LAST + HOPS:
                ops.append(("ring", q, stage))
        hop = tick - (NQ - 1) - LAST
        if hop == 0:
            ops.append(("down", 0, 0))
        elif 1 <= hop < HOPS:
            ops += [("down", 2 * hop - 1, NZ - hop), ("down", 2 * hop, hop)]
        elif hop == HOPS:
            ops.append(("down", NZ - 1, HOPS))
    return ops


def kernel(
    codes_hbm, scales_hbm, gate_hbm, up_hbm, down_hbm, out_ref,
    codes, scales, staged, swapped, acts, w, wd, part, ring, hidden, outs, finals,
    in_sem, w_local, w_send, w_recv, swap_sem, a_send, a_recv, r_send, r_recv, h_send, h_recv, f_send, f_recv,
):
    row, col = lax.axis_index("row"), lax.axis_index("col")
    z, core = row // CORES, row % CORES
    y, x = col // NX, col % NX
    other = 1 - core

    def along_z(step):
        return ((z + NZ + step) % NZ * CORES + core, col)

    def in_plane(sx, sy):
        return (row, (y + NY + sy) % NY * NX + (x + NX + sx) % NX)

    partner = (z * CORES + other, col)
    neighbours = (along_z(1), along_z(-1), in_plane(1, 0), in_plane(-1, 0), in_plane(0, 1), in_plane(0, -1))

    def remote(src, dst, send, recv, device):
        return pltpu.make_async_remote_copy(
            src_ref=src, dst_ref=dst, send_sem=send, recv_sem=recv, device_id=device, device_id_type=MESH
        )

    in_codes = pltpu.make_async_copy(codes_hbm, codes, in_sem.at[0])
    in_scales = pltpu.make_async_copy(scales_hbm, scales, in_sem.at[1])
    in_codes.start()
    in_scales.start()

    low = pl.ds(pl.multiple_of(core * LOW, 128), LOW)
    tail = pl.ds(pl.multiple_of(CORES * LOW + core * (D_ROW - LOW), 64), D_ROW - LOW)
    pieces = [
        (gate_hbm.at[pl.ds(0, LOW)], w.at[low, pl.ds(0, FF)]),
        (gate_hbm.at[pl.ds(LOW, D_ROW - LOW)], w.at[tail, pl.ds(0, FF)]),
        (up_hbm.at[pl.ds(0, LOW)], w.at[low, pl.ds(FF, FF)]),
        (up_hbm.at[pl.ds(LOW, D_ROW - LOW)], w.at[tail, pl.ds(FF, FF)]),
        (down_hbm, wd.at[core]),
    ]
    local = [pltpu.make_async_copy(src, dst, w_local.at[i]) for i, (src, dst) in enumerate(pieces)]
    pushed = [remote(src, dst, w_send.at[i], w_recv.at[i], partner) for i, (src, dst) in enumerate(pieces)]
    for copy in local:
        copy.start()

    barrier = pltpu.get_barrier_semaphore()
    for device in (partner, *neighbours):
        pl.semaphore_signal(barrier, inc=1, device_id=device, device_id_type=MESH)

    in_codes.wait()
    in_scales.wait()
    lane = lax.broadcasted_iota(jnp.int32, (TOK, 128), 1)
    for tile in range(D_ROW // 128):
        cut = pl.ds(tile * 128, 128)
        scale = jnp.where(
            lane < QB, scales[:, 2 * tile : 2 * tile + 1], scales[:, 2 * tile + 1 : 2 * tile + 2]
        )
        staged[:, cut] = (codes[:, cut].astype(F32) * scale).astype(BF16)
    last = codes[:, LOW:D_ROW].astype(F32) * scales[:, 6:7]
    staged[:, LOW:PAD] = jnp.concatenate([last, jnp.zeros_like(last)], axis=1).astype(BF16)

    pl.semaphore_wait(barrier, 1 + len(neighbours))
    swap = remote(
        staged.at[pl.ds(pl.multiple_of(other * HALF, HALF), HALF)], swapped, swap_sem.at[0], swap_sem.at[1], partner
    )
    swap.start()
    for copy in pushed:
        copy.start()
    swap.wait_recv()
    mine = staged[pl.ds(pl.multiple_of(core * HALF, HALF), HALF), :].astype(F32)
    theirs = swapped[...].astype(F32)
    first = jnp.where(core == 0, mine, theirs)
    second = jnp.where(core == 0, theirs, mine)
    acts[0:HALF, 0:LOW] = first[:, 0:LOW].astype(BF16)
    acts[0:HALF, LOW : 2 * LOW] = second[:, 0:LOW].astype(BF16)
    acts[0:HALF, 2 * LOW : D_CHIP] = (first[:, LOW:PAD] + pltpu.roll(second[:, LOW:PAD], QB, 1)).astype(BF16)

    def acts_rows(slot, half):
        return acts.at[pl.ds(SLOT[slot] * HALF + half * PIECE, PIECE)]

    def pass_on(slot, half):
        for sx, sy in steps_of(half, slot):
            there = ((slot[0] + sx) % NX, (slot[1] + sy) % NY)
            remote(
                acts_rows(slot, half), acts_rows(there, half), a_send, a_recv.at[half, SLOT[there]], in_plane(sx, sy)
            ).start()

    for half in range(2):
        pass_on((0, 0), half)

    def take_acts(slot):
        for half in range(2):
            rows = acts_rows(slot, half)
            remote(rows, rows, a_send, a_recv.at[half, SLOT[slot]], partner).wait_recv()
            pass_on(slot, half)

    def multiply(q):
        if q == 0:
            for i in range(4):
                local[i].wait()
                pushed[i].wait_recv()

        def tile(n, carry):
            cut = pl.ds(pl.multiple_of(n * 256, 256), 256)
            part[q, :, cut] = jnp.dot(
                acts[q * ROWS : (q + 1) * ROWS, :], w[:, cut], preferred_element_type=F32
            ).astype(BF16)
            return carry

        lax.fori_loop(0, GU // 256, tile, 0)

    def strip(q, d, owner):
        return part.at[q, pl.ds(pl.multiple_of(owner * PIECE + d * STRIP, STRIP), STRIP)]

    def arrived(ref, sem):
        remote(ref, ref, r_send, sem, partner).wait_recv()

    def piece(owner, q):
        return hidden.at[owner, pl.ds(q * PIECE, PIECE)]

    def ring_step(q, stage):
        for d in range(2):
            toward = 1 if d == 0 else -1
            if stage < LAST:
                owner = (z + NZ - toward * (stage + 1)) % NZ
                src = strip(q, d, owner)
                if stage > 0:
                    got = ring.at[d, q, stage - 1]
                    arrived(got, r_recv.at[d, q, stage - 1])
                    got[...] = (got[...].astype(F32) + src[...].astype(F32)).astype(BF16)
                    src = got
                remote(src, ring.at[d, q, stage], r_send, r_recv.at[d, q, stage], along_z(toward)).start()
            elif stage == LAST:
                got = ring.at[d, q, stage - 1]
                arrived(got, r_recv.at[d, q, stage - 1])
                own = strip(q, d, z)
                gate = got[:, 0:FF].astype(F32) + own[:, 0:FF].astype(F32)
                up = got[:, FF:GU].astype(F32) + own[:, FF:GU].astype(F32)
                value = gate / (1.0 + jnp.exp(-gate)) * up
                hidden[z, pl.ds(q * PIECE + d * STRIP, STRIP), :] = value.astype(BF16)
        if stage >= LAST:
            hop = stage - LAST
            for d in range(2):
                toward = 1 if d == 0 else -1
                if hop > max_hop(d, q):
                    continue
                ref = piece((z + NZ - toward * hop) % NZ, q)
                if hop > 0:
                    arrived(ref, h_recv.at[d, q, hop - 1])
                if hop < max_hop(d, q):
                    remote(ref, ref, h_send, h_recv.at[d, q, hop], along_z(toward)).start()

    def lookup(q, k, axis):
        packed = sum(s[axis] * 4**i for i, s in enumerate(GROUPS[q]))
        return packed // ((1 + 3 * (k % 2)) * (1 + 15 * (k // 2))) % 4

    def down(turn, offset):
        if turn == 0:
            local[4].wait()
            pushed[4].wait_recv()
        owner = (z + offset) % NZ
        for e in range(CORES):
            outs[turn, e, :, 0:D_ROW] = jnp.dot(
                hidden[owner], wd[e], preferred_element_type=F32
            ).astype(BF16)
        k = owner // 2
        to_rows = pl.ds(pl.multiple_of(core * HALF + owner % 2 * PIECE, PIECE), PIECE)
        for q in range(NQ):
            there = (y + NY - lookup(q, k, 1)) % NY * NX + (x + NX - lookup(q, k, 0)) % NX
            from_rows = pl.ds(q * PIECE, PIECE)

            def send(to_core, sem):
                remote(
                    outs.at[turn, to_core, from_rows],
                    finals.at[q * 4 + k, to_rows],
                    f_send,
                    f_recv.at[sem],
                    (z * CORES + to_core, there),
                ).start()

            if q > 0:
                for e in range(CORES):
                    send(e, 1)
                continue

            @pl.when(k == 0)
            def _():
                send(other, 0)
                finals[0, to_rows, :] = outs[turn, core, from_rows, :]

            @pl.when(k != 0)
            def _():
                send(other, 1)
                send(core, 1)

    act = {"acts": take_acts, "up": multiply, "ring": ring_step, "down": down}
    for name, *at in order():
        act[name](*at)

    def all_of(ref, send, recv):
        return remote(ref, ref, send, recv, partner)

    rest = finals.at[pl.ds(1, NX * NY - 1)]
    near = finals.at[0, pl.ds(pl.multiple_of(other * HALF, HALF), HALF)]
    all_of(near, f_send, f_recv.at[0]).wait_recv()
    all_of(rest, f_send, f_recv.at[1]).wait_recv()

    def total(i, carry):
        rows = pl.ds(pl.multiple_of(i * 16, 16), 16)
        value = finals[0, rows, :].astype(F32)
        for k in range(1, NX * NY):
            value = value + finals[k, rows, :].astype(F32)
        out_ref[rows, :] = value[:, 0:D_ROW].astype(out_ref.dtype)
        return carry

    lax.fori_loop(0, TOK // 16, total, 0)

    swap.wait_send()
    for copy in pushed:
        copy.wait_send()
    all_of(acts.at[pl.ds(HALF, 15 * HALF)], a_send, r_send).wait_send()
    all_of(ring, r_send, h_send).wait_send()
    all_of(hidden.at[pl.ds(0, NZ - 1)], h_send, r_send).wait_send()
    all_of(rest, f_send, r_send).wait_send()
    all_of(near, f_send, r_send).wait_send()


def solution(mesh):
    def step(act_codes, act_scales, gate_weight, up_weight, down_weight):
        dma = pltpu.SemaphoreType.DMA
        return pl.pallas_call(
            kernel,
            out_shape=jax.ShapeDtypeStruct((TOK, D_ROW), BF16),
            in_specs=[pl.BlockSpec(memory_space=pl.ANY)] * 5,
            out_specs=pl.BlockSpec(memory_space=pltpu.VMEM),
            scratch_shapes=[
                pltpu.VMEM((TOK, D_ROW), jnp.int32),
                pltpu.VMEM((TOK, 7), F32),
                pltpu.VMEM((TOK, PAD), BF16),
                pltpu.VMEM((HALF, PAD), BF16),
                pltpu.VMEM((NX * NY * HALF, D_CHIP), BF16),
                pltpu.VMEM((D_CHIP, GU), BF16),
                pltpu.VMEM((CORES, FF, D_ROW), BF16),
                pltpu.VMEM((NQ, ROWS, GU), BF16),
                pltpu.VMEM((2, NQ, LAST, STRIP, GU), BF16),
                pltpu.VMEM((NZ, NQ * PIECE, FF), BF16),
                pltpu.VMEM((NZ, CORES, NQ * PIECE, PAD), BF16),
                pltpu.VMEM((NX * NY, TOK, PAD), BF16),
                dma((2,)),
                dma((5,)),
                dma((5,)),
                dma((5,)),
                dma((2,)),
                dma,
                dma((2, NX * NY)),
                dma,
                dma((2, NQ, LAST)),
                dma,
                dma((2, NQ, HOPS)),
                dma,
                dma((2,)),
            ],
            compiler_params=pltpu.CompilerParams(
                collective_id=0, has_side_effects=True, vmem_limit_bytes=60 * 1024 * 1024
            ),
        )(act_codes, act_scales, gate_weight, up_weight, down_weight)

    return jax.shard_map(
        step,
        mesh=mesh,
        in_specs=(P("col", "row"), P("col", "row"), P("row", "col"), P("row", "col"), P("col", "row")),
        out_specs=P("col", "row"),
        check_vma=False,
    )
```

time: 234 us -> 121 us (0.52)
  waiting for transfers between devices: 128 us -> 0 us
  Pallas kernels: 0 us -> 114 us
  blocking collectives: 63.6 us -> 0 us
  between operations: 13.2 us -> 0.01 us
  matrix products: 11.2 us -> 0 us
  other arithmetic: 8.02 us -> 0 us
    pallas_call x0 -> x1, Pallas kernels: none -> 114 us  [step(): pl.pallas_call(kernel, out_shape=jax.ShapeDtypeStruct((TOK, D_ROW), BF16)...]
    reduce_scatter x2 -> x0, waiting for transfers between devices: 86.9 us -> none  [own_block(): tiles = lax.psum_scatter(tiles, axes[k], scatter_dimension=0, tiled=True)]
    all_to_all x2 -> x0, blocking collectives: 63.6 us -> none  [the longest x1 32.1 us: sent_to_all(): return lax.all_to_all(copies, axis, split_axis=0, concat_axis=0, tiled=True)]
    all_gather x1 -> x0, waiting for transfers between devices: 41.5 us -> none  [on_device(): lax.all_gather(hidden, ROW, axis=0, tiled=True)]
    dot_general x3 -> x0, matrix products: 11.2 us -> none  [the longest x1 4.9 us: on_device(): jnp.dot(lax.all_gather(hidden, ROW, axis=0, tiled=True), down_weight, pre...]
    transpose x1 -> x0, local copies, waits for them, and re-layouts: 8.14 us -> none  [own_block(): tiles = tiles.transpose(*order, *range(len(axes), tiles.ndim))]
    unnamed x6 -> x3, local copies, waits for them, and re-layouts: 0.01 us -> 5.62 us
    transpose x1 -> x0, other arithmetic: 4.02 us -> none  [own_block(): tiles = tiles.transpose(*order, *range(len(axes), tiles.ndim))]
  transfers between devices with their start and end apart: 3 -> 0, of which waited for: 3 -> 0; matrix products, arithmetic and copies ran while one was open for 0% -> 0% of each run, Pallas kernels for 0% -> 0%
where the time goes in v1:
time: 121 us
  Pallas kernels  114 us (94%)
  local copies, waits for them, and re-layouts  7.29 us (6%)
    pallas_call x1, Pallas kernels, step(): pl.pallas_call(kernel, out_shape=jax.ShapeDtypeStruct((TOK, D_ROW), BF16)...  114 us
    unnamed x3, local copies, waits for them, and re-layouts  5.62 us

profile of v1, /device:TPU:1, one launch (start us, length us, event | category | flops | bytes accessed | tf_op | source)
XLA Modules:
  0.0 120.9 jit_solution(12334176577987220368)
XLA Ops:
  0.0 1.4 %copy.7.scales_hbm = f32[128,7]{1,0:T(8,128)} copy(f32[128,7]{0,1:T(8,128)} %param.6) | data formatting | bytes 7168 | tf_op args[1]
  1.4 1.8 %copy.6.codes_hbm = s32[128,448]{1,0:T(8,128)} copy(s32[128,448]{0,1:T(8,128)} %param.5) | data formatting | bytes 458752 | tf_op args[0]
  3.2 2.4 %copy.8.down_hbm = bf16[1152,448]{1,0:T(8,128)(2,1)} copy(bf16[1152,448]{0,1:T(8,128)(2,1)} %param.9) | data formatting | bytes 2064384 | tf_op args[4]
  5.6 113.6 %shard_map.55 = bf16[128,448]{1,0:T(8,128)(2,1)} custom-call(s32[128,448]{1,0:T(8,128)} %copy.6.codes_hbm, f32[128,7]{1,0:T(8,128)} %copy.7.scales_hbm, bf16[448,1152]{1,0:T(8,128)(2,1)} %gate_hbm.1, bf16[448,1152]{1,0:T(8,128)(2,1)} %up_hbm.1, bf16[1152,448]{1,0:T(8,128)(2,1)} %copy.8.down_hbm), custom_call_target="tpu_custom_call" | custom-call | tf_op jit(solution)/shard_map/pallas_call | solution.py:312
  119.2 1.7 %copy.9 = bf16[128,448]{0,1:T(8,128)(2,1)} copy(bf16[128,448]{1,0:T(8,128)(2,1)} %shard_map.55) | data formatting | bytes 229376 | tf_op jit(solution)/shard_map/pallas_call | solution.py:312

commit v2 on v1

v2 whole, which is shorter than its diff:
```python
import functools

import jax
import jax.numpy as jnp
from jax import lax
from jax.experimental import pallas as pl
from jax.experimental.pallas import tpu as pltpu
from jax.sharding import PartitionSpec as P

MESH = pl.DeviceIdType.MESH
F32 = jnp.float32
BF16 = jnp.bfloat16

NZ, NX, NY, CORES = 8, 4, 4, 2
TOK = 128
HALF = TOK // CORES
D_ROW = 448
LOW = 384
D_CHIP = CORES * D_ROW
FF = 1152
GU = 2 * FF
PAD = 512
PIECE = 32
STRIP = 16
QB = 64

GROUPS = (
    ((0, 0), (1, 0), (3, 0), (0, 1)),
    ((0, 3), (1, 1), (3, 3), (1, 3)),
    ((3, 1), (2, 0), (0, 2), (2, 1)),
    ((1, 2), (3, 2), (2, 3), (2, 2)),
)
TURNS = (0, 1, 0, 2, 3, 2, 0, 1, 3, 2, 1, 3, 2, 1, 3, 2, 0, 3, 1, 2, 0, 3, 1, 2, 0, 3, 1, 2, 0, 3, 1, 2, 0, 3, 1, 0)
NQ = len(GROUPS)
SLOT = {s: i for i, s in enumerate(s for g in GROUPS for s in g)}
ROWS = HALF * 4
PASS_ON = {
    (0, 0): ((1, 0), (-1, 0), (0, 1), (0, -1)),
    (1, 0): ((0, 1), (0, -1), (1, 0)),
    (3, 0): ((0, 1), (0, -1)),
    (0, 1): ((0, 1),),
    (1, 1): ((0, 1),),
    (3, 3): ((0, -1),),
    (2, 0): ((0, 1), (0, -1)),
    (2, 3): ((0, -1),),
}
HOPS = NZ // 2
LAST = HOPS


def steps_of(part, slot):
    if part == 0:
        return PASS_ON.get(slot, ())
    return tuple((b, a) for a, b in PASS_ON.get((slot[1], slot[0]), ()))


def length(d, strip):
    return HOPS if strip == d else HOPS - 1


def place(d, strip, hop):
    return hop if strip == d else HOPS + hop


def order():
    near = ((1, 0), (3, 0), (0, 1), (0, 3))
    taken = {(0, 0)}
    ops = []

    def take(slots, late):
        for slot in slots:
            if slot not in taken:
                ops.append(("take", slot, late))
                taken.add(slot)

    at = [0] * NQ
    for q in TURNS:
        stage, at[q] = at[q], at[q] + 1
        if stage == 0:
            if q == 0:
                take(near, True)
                ops += [("pass_on", slot, False) for slot in near]
            take(GROUPS[q], False)
            if q == TURNS[0]:
                ops.append(("weights", 0, 4))
            ops.append(("up", q))
            continue
        ops.append(("ring", q, stage))
        if stage >= LAST:
            if not any(op[0] == "down" for op in ops):
                ops.append(("weights", 4, 5))
            ops.append(("down", q, stage - LAST))
    return ops


def kernel(
    codes, scales, gate_hbm, up_hbm, down_hbm, out_ref,
    staged, swapped, acts, w, wd, part, ring, hidden, outs, finals,
    w_local, w_send, w_recv, swap_sem, a_send, a_recv, r_send, r_recv, h_send, h_recv, f_send, f_recv,
):
    row, col = lax.axis_index("row"), lax.axis_index("col")
    z, core = row // CORES, row % CORES
    y, x = col // NX, col % NX
    other = 1 - core

    def along_z(step):
        return ((z + NZ + step) % NZ * CORES + core, col)

    def in_plane(sx, sy):
        return (row, (y + NY + sy) % NY * NX + (x + NX + sx) % NX)

    partner = (z * CORES + other, col)
    neighbours = (along_z(1), along_z(-1), in_plane(1, 0), in_plane(-1, 0), in_plane(0, 1), in_plane(0, -1))

    def remote(src, dst, send, recv, device):
        return pltpu.make_async_remote_copy(
            src_ref=src, dst_ref=dst, send_sem=send, recv_sem=recv, device_id=device, device_id_type=MESH
        )

    low = pl.ds(pl.multiple_of(core * LOW, 128), LOW)
    tail = pl.ds(pl.multiple_of(CORES * LOW + core * (D_ROW - LOW), 64), D_ROW - LOW)
    pieces = [
        (gate_hbm.at[pl.ds(0, LOW)], w.at[low, pl.ds(0, FF)]),
        (gate_hbm.at[pl.ds(LOW, D_ROW - LOW)], w.at[tail, pl.ds(0, FF)]),
        (up_hbm.at[pl.ds(0, LOW)], w.at[low, pl.ds(FF, FF)]),
        (up_hbm.at[pl.ds(LOW, D_ROW - LOW)], w.at[tail, pl.ds(FF, FF)]),
        (down_hbm, wd.at[core]),
    ]
    local = [pltpu.make_async_copy(src, dst, w_local.at[i]) for i, (src, dst) in enumerate(pieces)]
    pushed = [remote(src, dst, w_send.at[i], w_recv.at[i], partner) for i, (src, dst) in enumerate(pieces)]
    for copy in local:
        copy.start()

    barrier = pltpu.get_barrier_semaphore()
    for device in (partner, *neighbours):
        pl.semaphore_signal(barrier, inc=1, device_id=device, device_id_type=MESH)

    blocks = [
        codes[QB * k : QB * (k + 1), :].astype(F32) * scales[k : k + 1, :] for k in range(D_ROW // QB)
    ]
    blocks.append(jnp.zeros_like(blocks[0]))
    for tile in range(PAD // 128):
        pair = jnp.concatenate(blocks[2 * tile : 2 * tile + 2], axis=0)
        staged[:, tile * 128 : (tile + 1) * 128] = pair.T.astype(BF16)

    pl.semaphore_wait(barrier, 1 + len(neighbours))
    swap = remote(
        staged.at[pl.ds(pl.multiple_of(other * HALF, HALF), HALF)], swapped, swap_sem.at[0], swap_sem.at[1], partner
    )
    swap.start()
    for copy in pushed:
        copy.start()
    swap.wait_recv()
    mine = staged[pl.ds(pl.multiple_of(core * HALF, HALF), HALF), :].astype(F32)
    theirs = swapped[...].astype(F32)
    first = jnp.where(core == 0, mine, theirs)
    second = jnp.where(core == 0, theirs, mine)
    acts[0:HALF, 0:LOW] = first[:, 0:LOW].astype(BF16)
    acts[0:HALF, LOW : 2 * LOW] = second[:, 0:LOW].astype(BF16)
    acts[0:HALF, 2 * LOW : D_CHIP] = (first[:, LOW:PAD] + pltpu.roll(second[:, LOW:PAD], QB, 1)).astype(BF16)

    def acts_rows(slot, half):
        return acts.at[pl.ds(SLOT[slot] * HALF + half * PIECE, PIECE)]

    def pass_on(slot, urgent):
        for half in range(2):
            for sx, sy in steps_of(half, slot):
                there = ((slot[0] + sx) % NX, (slot[1] + sy) % NY)
                if urgent is None or (there in GROUPS[1]) == urgent:
                    remote(
                        acts_rows(slot, half),
                        acts_rows(there, half),
                        a_send,
                        a_recv.at[half, SLOT[there]],
                        in_plane(sx, sy),
                    ).start()

    pass_on((0, 0), None)

    def take_acts(slot, late):
        for half in range(2):
            rows = acts_rows(slot, half)
            remote(rows, rows, a_send, a_recv.at[half, SLOT[slot]], partner).wait_recv()
        pass_on(slot, True if late else None)

    def multiply(q):
        for cut in (pl.ds(0, FF), pl.ds(FF, FF)):
            part[q, :, cut] = jnp.dot(
                acts[q * ROWS : (q + 1) * ROWS, :], w[:, cut], preferred_element_type=F32
            ).astype(BF16)
            for d in range(2):
                for strip in range(2):
                    remote(
                        rows_of(q, strip, z_at(d, length(d, strip))).at[:, cut],
                        ring.at[d, q, place(d, strip, 0), :, cut],
                        r_send,
                        r_recv.at[d, q, place(d, strip, 0)],
                        along_z(toward(d)),
                    ).start()

    def toward(d):
        return 1 - 2 * d

    def z_at(d, hops):
        return (z + NZ + toward(d) * hops) % NZ

    def rows_of(q, strip, owner):
        return part.at[q, pl.ds(pl.multiple_of(owner * PIECE + strip * STRIP, STRIP), STRIP)]

    def arrived(ref, sem):
        remote(ref, ref, r_send, sem, partner).wait_recv()

    def received(q, d, strip, hop):
        ref = ring.at[d, q, place(d, strip, hop)]
        arrived(ref, r_recv.at[d, q, place(d, strip, hop)])
        return ref

    def piece(owner, q):
        return hidden.at[owner, pl.ds(q * PIECE, PIECE)]

    def gather_step(q, hop):
        for d in range(2):
            ref = piece(z_at(d, -hop), q)
            half = hidden.at[z_at(d, -hop), pl.ds(q * PIECE + d * STRIP, STRIP)]
            if hop > 0:
                came = ref if hop < HOPS else half
                arrived(came, h_recv.at[d, q, hop - 1])
            if hop < HOPS:
                goes = ref if hop < HOPS - 1 else half
                remote(goes, goes, h_send, h_recv.at[d, q, hop], along_z(toward(d))).start()

    def ring_step(q, stage):
        if stage < LAST:
            for d in range(2):
                for strip in range(2):
                    left = length(d, strip) - stage
                    if left <= 0:
                        continue
                    got = received(q, d, strip, stage - 1)
                    got[...] = (got[...].astype(F32) + rows_of(q, strip, z_at(d, left))[...].astype(F32)).astype(BF16)
                    at = place(d, strip, stage)
                    remote(got, ring.at[d, q, at], r_send, r_recv.at[d, q, at], along_z(toward(d))).start()
            return
        if stage == LAST:
            for strip in range(2):
                a, b = (received(q, d, strip, length(d, strip) - 1) for d in range(2))
                own = rows_of(q, strip, z)
                gate, up = (
                    a[:, cut].astype(F32) + b[:, cut].astype(F32) + own[:, cut].astype(F32)
                    for cut in (pl.ds(0, FF), pl.ds(FF, FF))
                )
                value = gate / (1.0 + jnp.exp(-gate)) * up
                hidden[z, pl.ds(q * PIECE + strip * STRIP, STRIP), :] = value.astype(BF16)
        gather_step(q, stage - LAST)

    def lookup(q, k, axis):
        packed = sum(s[axis] * 4**i for i, s in enumerate(GROUPS[q]))
        return packed // ((1 + 3 * (k % 2)) * (1 + 15 * (k // 2))) % 4

    def down(q, hop):
        if hop == 0:
            turns = [(0, z)]
        elif hop < HOPS:
            turns = [(2 * hop - 1, (z + NZ - hop) % NZ), (2 * hop, (z + hop) % NZ)]
        else:
            turns = [(NZ - 1, (z + HOPS) % NZ)]
        from_rows = pl.ds(q * PIECE, PIECE)
        value = jnp.concatenate([hidden[owner, from_rows, :] for _, owner in turns], axis=0)
        for e in range(CORES):
            product = lax.dot_general(
                value, wd[e], (((1,), (1,)), ((), ())), preferred_element_type=F32
            ).astype(BF16)
            for i, (turn, _) in enumerate(turns):
                outs[turn, e, from_rows, 0:D_ROW] = product[i * PIECE : (i + 1) * PIECE]
        for turn, owner in turns:
            k = owner // 2
            to_rows = pl.ds(pl.multiple_of(core * HALF + owner % 2 * PIECE, PIECE), PIECE)
            there = (y + NY - lookup(q, k, 1)) % NY * NX + (x + NX - lookup(q, k, 0)) % NX

            def send(to_core, sem):
                remote(
                    outs.at[turn, to_core, from_rows],
                    finals.at[q * 4 + k, to_rows],
                    f_send,
                    f_recv.at[sem],
                    (z * CORES + to_core, there),
                ).start()

            if q > 0:
                for e in range(CORES):
                    send(e, 1)
                continue

            @pl.when(k == 0)
            def _():
                send(other, 0)
                finals[0, to_rows, :] = outs[turn, core, from_rows, :]

            @pl.when(k != 0)
            def _():
                send(other, 1)
                send(core, 1)

    def weights(first, end):
        for i in range(first, end):
            local[i].wait()
            pushed[i].wait_recv()

    act = {"weights": weights, "take": take_acts, "pass_on": pass_on, "up": multiply, "ring": ring_step, "down": down}
    for name, *at in order():
        act[name](*at)

    def all_of(ref, send, recv):
        return remote(ref, ref, send, recv, partner)

    rest = finals.at[pl.ds(1, NX * NY - 1)]
    near = finals.at[0, pl.ds(pl.multiple_of(other * HALF, HALF), HALF)]
    all_of(near, f_send, f_recv.at[0]).wait_recv()
    all_of(rest, f_send, f_recv.at[1]).wait_recv()

    for tile in range(PAD // 128):
        cut = pl.ds(tile * 128, 128)
        value = finals[0, :, cut].astype(F32)
        for k in range(1, NX * NY):
            value = value + finals[k, :, cut].astype(F32)
        rows = min(128, D_ROW - tile * 128)
        out_ref[tile * 128 : tile * 128 + rows, :] = value.T[0:rows, :].astype(out_ref.dtype)

    swap.wait_send()
    for copy in pushed:
        copy.wait_send()
    all_of(acts.at[pl.ds(HALF, 15 * HALF)], a_send, r_send).wait_send()
    all_of(ring, r_send, h_send).wait_send()
    all_of(hidden.at[pl.ds(0, NZ - 1)], h_send, r_send).wait_send()
    all_of(rest, f_send, r_send).wait_send()
    all_of(near, f_send, r_send).wait_send()


def solution(mesh):
    def step(act_codes, act_scales, gate_weight, up_weight, down_weight):
        dma = pltpu.SemaphoreType.DMA
        return pl.pallas_call(
            kernel,
            out_shape=jax.ShapeDtypeStruct((D_ROW, TOK), BF16),
            in_specs=[pl.BlockSpec(memory_space=pltpu.VMEM)] * 2 + [pl.BlockSpec(memory_space=pltpu.HBM)] * 3,
            out_specs=pl.BlockSpec(memory_space=pltpu.VMEM),
            scratch_shapes=[
                pltpu.VMEM((TOK, PAD), BF16),
                pltpu.VMEM((HALF, PAD), BF16),
                pltpu.VMEM((NX * NY * HALF, D_CHIP), BF16),
                pltpu.VMEM((D_CHIP, GU), BF16),
                pltpu.VMEM((CORES, D_ROW, FF), BF16),
                pltpu.VMEM((NQ, ROWS, GU), BF16),
                pltpu.VMEM((2, NQ, NZ - 1, STRIP, GU), BF16),
                pltpu.VMEM((NZ, NQ * PIECE, FF), BF16),
                pltpu.VMEM((NZ, CORES, NQ * PIECE, PAD), BF16),
                pltpu.VMEM((NX * NY, TOK, PAD), BF16),
                dma((5,)),
                dma((5,)),
                dma((5,)),
                dma((2,)),
                dma,
                dma((2, NX * NY)),
                dma,
                dma((2, NQ, NZ - 1)),
                dma,
                dma((2, NQ, HOPS)),
                dma,
                dma((2,)),
            ],
            compiler_params=pltpu.CompilerParams(
                collective_id=0, has_side_effects=True, vmem_limit_bytes=56_000_000
            ),
        )(act_codes.T, act_scales.T, gate_weight, up_weight, down_weight.T).T

    return jax.shard_map(
        step,
        mesh=mesh,
        in_specs=(P("col", "row"), P("col", "row"), P("row", "col"), P("row", "col"), P("col", "row")),
        out_specs=P("col", "row"),
        check_vma=False,
    )
```

time: 121 us -> 97.2 us (0.80)
  Pallas kernels: 114 us -> 94.8 us
  local copies, waits for them, and re-layouts: 7.29 us -> 2.27 us
    pallas_call x1, Pallas kernels: 114 us -> 94.8 us  [step(): pl.pallas_call(kernel, out_shape=jax.ShapeDtypeStruct((D_ROW, TOK), BF16)...]
    unnamed x3 -> x5, local copies, waits for them, and re-layouts: 5.62 us -> 2.27 us
    pallas_call x1 -> x0, local copies, waits for them, and re-layouts: 1.67 us -> none  [step(): pl.pallas_call(kernel, out_shape=jax.ShapeDtypeStruct((TOK, D_ROW), BF16)...]
where the time goes in v2:
time: 97.2 us; the launch traced here: 97 us
  Pallas kernels  94.8 us (98%)
  local copies, waits for them, and re-layouts  2.27 us (2%)
    pallas_call x1, Pallas kernels, step(): pl.pallas_call(kernel, out_shape=jax.ShapeDtypeStruct((D_ROW, TOK), BF16)...  94.8 us
    unnamed x5, local copies, waits for them, and re-layouts  2.27 us

profile of v2, /device:TPU:1, one launch (start us, length us, event | category | flops | bytes accessed | tf_op | source)
XLA Modules:
  0.0 97.0 jit_solution(3848777484346680627)
XLA Ops:
  0.0 0.0 copy-start.1
  0.0 0.7 copy-done.1
  0.7 0.0 copy-start
  0.7 0.9 copy-done
  1.6 94.8 %shard_map.55 = bf16[448,128]{1,0:T(8,128)(2,1)S(1)} custom-call(s32[448,128]{1,0:T(8,128)S(1)} %bitcast.5, f32[7,128]{1,0:T(8,128)S(1)} %bitcast.6, bf16[448,1152]{1,0:T(8,128)(2,1)} %gate_hbm.1, bf16[448,1152]{1,0:T(8,128)(2,1)} %up_hbm.1, bf16[448,1152]{1,0:T(8,128)(2,1)} %bitcast.7), custom_call_target="tpu_custom_call" | custom-call | tf_op jit(solution)/shard_map/pallas_call | solution.py:342
  96.4 0.6 copy.7
Async XLA Ops:
  0.0 0.7 copy-start.1
  0.7 0.9 copy-start

commit v3 on v2

v3 whole, which is shorter than its diff:
```python
import functools

import jax
import jax.numpy as jnp
from jax import lax
from jax.experimental import pallas as pl
from jax.experimental.pallas import tpu as pltpu
from jax.sharding import PartitionSpec as P

MESH = pl.DeviceIdType.MESH
F32 = jnp.float32
BF16 = jnp.bfloat16

NZ, NX, NY, CORES = 8, 4, 4, 2
TOK = 128
HALF = TOK // CORES
D_ROW = 448
LOW = 384
D_CHIP = CORES * D_ROW
FF = 1152
GU = 2 * FF
PAD = 512
PIECE = 32
STRIP = 16
QB = 64

GROUPS = (
    ((0, 0), (1, 0), (3, 0), (0, 1)),
    ((0, 3), (1, 1), (3, 3), (1, 3)),
    ((3, 1), (2, 0), (0, 2), (2, 1)),
    ((1, 2), (3, 2), (2, 3), (2, 2)),
)
TURNS = (0, 1, 0, 2, 3, 2, 0, 1, 3, 2, 1, 3, 2, 1, 3, 2, 0, 3, 1, 2, 0, 3, 1, 2, 0, 3, 1, 2, 0, 3, 1, 2, 0, 3, 1, 0)
NQ = len(GROUPS)
SLOT = {s: i for i, s in enumerate(s for g in GROUPS for s in g)}
ROWS = HALF * 4
PASS_ON = {
    (0, 0): ((1, 0), (-1, 0), (0, 1), (0, -1)),
    (1, 0): ((0, 1), (0, -1), (1, 0)),
    (3, 0): ((0, 1), (0, -1)),
    (0, 1): ((0, 1),),
    (1, 1): ((0, 1),),
    (3, 3): ((0, -1),),
    (2, 0): ((0, 1), (0, -1)),
    (2, 3): ((0, -1),),
}
HOPS = NZ // 2
LAST = HOPS


def steps_of(part, slot):
    if part == 0:
        return PASS_ON.get(slot, ())
    return tuple((b, a) for a, b in PASS_ON.get((slot[1], slot[0]), ()))


def strip_of(kind, d):
    return d if kind == 0 else 1 - d


def place(kind, hop):
    return kind * HOPS + hop


def order():
    near = ((1, 0), (3, 0), (0, 1), (0, 3))
    taken = {(0, 0)}
    ops = []

    def take(slots, late):
        for slot in slots:
            if slot not in taken:
                ops.append(("take", slot, late))
                taken.add(slot)

    at = [0] * NQ
    for q in TURNS:
        stage, at[q] = at[q], at[q] + 1
        if stage == 0:
            if q == 0:
                take(near, True)
                ops += [("pass_on", slot, False) for slot in near]
            take(GROUPS[q], False)
            if q == 2:
                take(GROUPS[3][:3], False)
            if q == TURNS[0]:
                ops.append(("weights", 0))
            ops.append(("up", q))
            continue
        ops.append(("ring", q, stage))
        if stage >= LAST:
            if not any(op[0] == "down" for op in ops):
                ops.append(("weights", 1))
            ops.append(("down", q, stage - LAST))
    return ops


def kernel(
    codes_hbm, scales_hbm, gate_hbm, up_hbm, down_hbm, out_ref,
    codes, scales, staged, swapped, acts, w, wd, part, ring, hidden, outs, finals,
    sent, in_sem, w_local, w_recv, swap_recv, a_recv, r_recv, h_recv, f_recv,
):
    row, col = lax.axis_index("row"), lax.axis_index("col")
    z, core = row // CORES, row % CORES
    y, x = col // NX, col % NX
    other = 1 - core

    def along_z(step):
        return ((z + NZ + step) % NZ * CORES + core, col)

    def in_plane(sx, sy):
        return (row, (y + NY + sy) % NY * NX + (x + NX + sx) % NX)

    partner = (z * CORES + other, col)
    neighbours = (along_z(1), along_z(-1), in_plane(1, 0), in_plane(-1, 0), in_plane(0, 1), in_plane(0, -1))

    def remote(src, dst, recv, device):
        return pltpu.make_async_remote_copy(
            src_ref=src, dst_ref=dst, send_sem=sent, recv_sem=recv, device_id=device, device_id_type=MESH
        )

    def arrived(ref, sem):
        remote(ref, ref, sem, partner).wait_recv()

    in_codes = pltpu.make_async_copy(codes_hbm, codes, in_sem.at[0])
    in_scales = pltpu.make_async_copy(scales_hbm, scales, in_sem.at[1])
    in_codes.start()
    in_scales.start()
    barrier = pltpu.get_barrier_semaphore()
    for device in (partner, *neighbours):
        pl.semaphore_signal(barrier, inc=1, device_id=device, device_id_type=MESH)

    low = pl.ds(pl.multiple_of(core * LOW, 128), LOW)
    tail = pl.ds(pl.multiple_of(CORES * LOW + core * (D_ROW - LOW), 64), D_ROW - LOW)
    pieces = [
        (gate_hbm.at[pl.ds(0, LOW)], w.at[low, pl.ds(0, FF)]),
        (gate_hbm.at[pl.ds(LOW, D_ROW - LOW)], w.at[tail, pl.ds(0, FF)]),
        (up_hbm.at[pl.ds(0, LOW)], w.at[low, pl.ds(FF, FF)]),
        (up_hbm.at[pl.ds(LOW, D_ROW - LOW)], w.at[tail, pl.ds(FF, FF)]),
        (down_hbm, wd.at[core]),
    ]
    for i, (src, dst) in enumerate(pieces):
        pltpu.make_async_copy(src, dst, w_local.at[i // 4]).start()

    in_codes.wait()
    in_scales.wait()
    blocks = [
        codes[QB * k : QB * (k + 1), :].astype(F32) * scales[k : k + 1, :] for k in range(D_ROW // QB)
    ]
    blocks.append(jnp.zeros_like(blocks[0]))
    for tile in range(PAD // 128):
        pair = jnp.concatenate(blocks[2 * tile : 2 * tile + 2], axis=0)
        staged[:, tile * 128 : (tile + 1) * 128] = pair.T.astype(BF16)

    pl.semaphore_wait(barrier, 1 + len(neighbours))
    swap = remote(
        staged.at[pl.ds(pl.multiple_of(other * HALF, HALF), HALF)], swapped, swap_recv, partner
    )
    swap.start()
    for i, (src, dst) in enumerate(pieces):
        remote(src, dst, w_recv.at[i // 4], partner).start()
    swap.wait_recv()
    mine = staged[pl.ds(pl.multiple_of(core * HALF, HALF), HALF), :].astype(F32)
    theirs = swapped[...].astype(F32)
    first = jnp.where(core == 0, mine, theirs)
    second = jnp.where(core == 0, theirs, mine)
    acts[0:HALF, 0:LOW] = first[:, 0:LOW].astype(BF16)
    acts[0:HALF, LOW : 2 * LOW] = second[:, 0:LOW].astype(BF16)
    acts[0:HALF, 2 * LOW : D_CHIP] = (first[:, LOW:PAD] + pltpu.roll(second[:, LOW:PAD], QB, 1)).astype(BF16)

    def acts_rows(slot, half):
        return acts.at[pl.ds(SLOT[slot] * HALF + half * PIECE, PIECE)]

    def pass_on(slot, urgent):
        for half in range(2):
            for sx, sy in steps_of(half, slot):
                there = ((slot[0] + sx) % NX, (slot[1] + sy) % NY)
                if urgent is None or (there in GROUPS[1]) == urgent:
                    remote(
                        acts_rows(slot, half),
                        acts_rows(there, half),
                        a_recv.at[SLOT[there]],
                        in_plane(sx, sy),
                    ).start()

    pass_on((0, 0), None)

    def take_acts(slot, late):
        arrived(acts.at[pl.ds(SLOT[slot] * HALF, HALF)], a_recv.at[SLOT[slot]])
        pass_on(slot, True if late else None)

    def multiply(q):
        for cut in (pl.ds(0, FF), pl.ds(FF, FF)):
            part[q, :, cut] = jnp.dot(
                acts[q * ROWS : (q + 1) * ROWS, :], w[:, cut], preferred_element_type=F32
            ).astype(BF16)
            for kind in range(2):
                for d in range(2):
                    at = place(kind, 0)
                    remote(
                        rows_of(q, strip_of(kind, d), z_at(d, HOPS - kind)).at[:, cut],
                        ring.at[q, at, d, :, cut],
                        r_recv.at[q, at],
                        along_z(toward(d)),
                    ).start()

    def toward(d):
        return 1 - 2 * d

    def z_at(d, hops):
        return (z + NZ + toward(d) * hops) % NZ

    def rows_of(q, strip, owner):
        return part.at[q, pl.ds(pl.multiple_of(owner * PIECE + strip * STRIP, STRIP), STRIP)]

    def received(q, at):
        arrived(ring.at[q, at], r_recv.at[q, at])

    def piece(owner, q):
        return hidden.at[owner, pl.ds(q * PIECE, PIECE)]

    def gather_step(q, hop):
        if hop > 0:
            both = 2 * (PIECE if hop < HOPS else STRIP)
            arrived(hidden.at[0, pl.ds(0, both)], h_recv.at[q, hop - 1])
        if hop < HOPS:
            for d in range(2):
                goes = piece(z_at(d, -hop), q)
                if hop == HOPS - 1:
                    goes = hidden.at[z_at(d, -hop), pl.ds(q * PIECE + d * STRIP, STRIP)]
                remote(goes, goes, h_recv.at[q, hop], along_z(toward(d))).start()

    def ring_step(q, stage):
        if stage < LAST:
            for kind in range(2):
                left = HOPS - kind - stage
                if left <= 0:
                    continue
                at = place(kind, stage)
                received(q, at - 1)
                for d in range(2):
                    got = ring.at[q, at - 1, d]
                    own = rows_of(q, strip_of(kind, d), z_at(d, left))
                    got[...] = (got[...].astype(F32) + own[...].astype(F32)).astype(BF16)
                    remote(got, ring.at[q, at, d], r_recv.at[q, at], along_z(toward(d))).start()
            return
        if stage == LAST:
            ends = [place(kind, HOPS - kind - 1) for kind in range(2)]
            for at in ends:
                received(q, at)
            for strip in range(2):
                a, b = ring.at[q, ends[0], strip], ring.at[q, ends[1], 1 - strip]
                own = rows_of(q, strip, z)
                gate, up = (
                    a[:, cut].astype(F32) + b[:, cut].astype(F32) + own[:, cut].astype(F32)
                    for cut in (pl.ds(0, FF), pl.ds(FF, FF))
                )
                value = gate / (1.0 + jnp.exp(-gate)) * up
                hidden[z, pl.ds(q * PIECE + strip * STRIP, STRIP), :] = value.astype(BF16)
        gather_step(q, stage - LAST)

    def lookup(q, k, axis):
        packed = sum(s[axis] * 4**i for i, s in enumerate(GROUPS[q]))
        return packed // ((1 + 3 * (k % 2)) * (1 + 15 * (k // 2))) % 4

    def down(q, hop):
        if hop == 0:
            turns = [(0, z)]
        elif hop < HOPS:
            turns = [(2 * hop - 1, (z + NZ - hop) % NZ), (2 * hop, (z + hop) % NZ)]
        else:
            turns = [(NZ - 1, (z + HOPS) % NZ)]
        from_rows = pl.ds(q * PIECE, PIECE)
        value = jnp.concatenate([hidden[owner, from_rows, :] for _, owner in turns], axis=0)

        def multiply_by(e):
            product = lax.dot_general(
                value, wd[e], (((1,), (1,)), ((), ())), preferred_element_type=F32
            ).astype(BF16)
            for i, (turn, _) in enumerate(turns):
                outs[turn, e, from_rows, 0:D_ROW] = product[i * PIECE : (i + 1) * PIECE]

        def goes_to(turn, owner):
            k = owner // 2
            to_rows = pl.ds(pl.multiple_of(core * HALF + owner % 2 * PIECE, PIECE), PIECE)
            there = (y + NY - lookup(q, k, 1)) % NY * NX + (x + NX - lookup(q, k, 0)) % NX

            def send(to_core, sem):
                remote(
                    outs.at[turn, to_core, from_rows],
                    finals.at[q * 4 + k, to_rows],
                    f_recv.at[sem],
                    (z * CORES + to_core, there),
                ).start()

            return k, to_rows, send

        for e in range(CORES):
            multiply_by(e)
        for turn, owner in turns:
            k, to_rows, send = goes_to(turn, owner)
            if q > 0:
                for e in range(CORES):
                    send(e, 1)
                continue

            @pl.when(k == 0)
            def _():
                send(other, 0)
                finals[0, to_rows, :] = outs[turn, core, from_rows, :]

            @pl.when(k != 0)
            def _():
                send(other, 1)
                send(core, 1)

    def weights(which):
        ref = w.at[pl.ds(0, D_ROW)] if which == 0 else wd.at[0]
        pltpu.make_async_copy(ref, ref, w_local.at[which]).wait()
        arrived(ref, w_recv.at[which])

    act = {"weights": weights, "take": take_acts, "pass_on": pass_on, "up": multiply, "ring": ring_step, "down": down}
    for name, *at in order():
        act[name](*at)

    rest = finals.at[pl.ds(1, NX * NY - 1)]
    near = finals.at[0, pl.ds(pl.multiple_of(other * HALF, HALF), HALF)]
    arrived(near, f_recv.at[0])
    arrived(rest, f_recv.at[1])

    for tile in range(PAD // 128):
        cut = pl.ds(tile * 128, 128)
        value = finals[0, :, cut].astype(F32)
        for k in range(1, NX * NY):
            value = value + finals[k, :, cut].astype(F32)
        rows = min(128, D_ROW - tile * 128)
        out_ref[tile * 128 : tile * 128 + rows, :] = value.T[0:rows, :].astype(out_ref.dtype)

    for ref in (
        swapped, w.at[pl.ds(0, D_ROW)], wd.at[0], acts.at[pl.ds(HALF, (NX * NY - 1) * HALF)], ring,
        hidden.at[pl.ds(0, NZ - 1)], rest, near,
    ):
        remote(ref, ref, swap_recv, partner).wait_send()


def solution(mesh):
    def step(act_codes, act_scales, gate_weight, up_weight, down_weight):
        dma = pltpu.SemaphoreType.DMA
        return pl.pallas_call(
            kernel,
            out_shape=pltpu.VMEM((D_ROW, TOK), BF16),
            in_specs=[pl.BlockSpec(memory_space=pltpu.HBM)] * 5,
            out_specs=pl.BlockSpec(memory_space=pltpu.VMEM),
            scratch_shapes=[
                pltpu.VMEM((D_ROW, TOK), jnp.int32),
                pltpu.VMEM((7, TOK), F32),
                pltpu.VMEM((TOK, PAD), BF16),
                pltpu.VMEM((HALF, PAD), BF16),
                pltpu.VMEM((NX * NY * HALF, D_CHIP), BF16),
                pltpu.VMEM((D_CHIP, GU), BF16),
                pltpu.VMEM((CORES, D_ROW, FF), BF16),
                pltpu.VMEM((NQ, ROWS, GU), BF16),
                pltpu.VMEM((NQ, NZ - 1, 2, STRIP, GU), BF16),
                pltpu.VMEM((NZ, NQ * PIECE, FF), BF16),
                pltpu.VMEM((NZ, CORES, NQ * PIECE, PAD), BF16),
                pltpu.VMEM((NX * NY, TOK, PAD), BF16),
                dma,
                dma((2,)),
                dma((2,)),
                dma((2,)),
                dma,
                dma((NX * NY,)),
                dma((NQ, NZ - 1)),
                dma((NQ, HOPS)),
                dma((2,)),
            ],
            compiler_params=pltpu.CompilerParams(
                collective_id=0, has_side_effects=True, vmem_limit_bytes=56_000_000
            ),
        )(*(
            pltpu.with_memory_space_constraint(array, pltpu.HBM)
            for array in (act_codes.T, act_scales.T, gate_weight, up_weight, down_weight.T)
        )).T

    return jax.shard_map(
        step,
        mesh=mesh,
        in_specs=(P("col", "row"), P("col", "row"), P("row", "col"), P("row", "col"), P("col", "row")),
        out_specs=P("col", "row"),
        check_vma=False,
    )
```

time: 97.2 us -> 94.7 us (0.974)
  local copies, waits for them, and re-layouts: 2.27 us -> 0.65 us
    unnamed x5 -> x1, local copies, waits for them, and re-layouts: 2.27 us -> 0.65 us
where the time goes in v3:
time: 94.7 us
  Pallas kernels  94 us (99%)
    pallas_call x1, Pallas kernels, step(): pl.pallas_call(kernel, out_shape=pltpu.VMEM((D_ROW, TOK), BF16), in_specs...  94 us

profile of v3, /device:TPU:1, one launch (start us, length us, event | category | flops | bytes accessed | tf_op | source)
XLA Modules:
  0.0 94.7 jit_solution(966239485932102905)
XLA Ops:
  0.0 94.0 %shard_map.55 = bf16[448,128]{1,0:T(8,128)(2,1)S(1)} custom-call(s32[448,128]{1,0:T(8,128)} %bitcast.6, f32[7,128]{1,0:T(8,128)} %bitcast.7, bf16[448,1152]{1,0:T(8,128)(2,1)} %gate_hbm.1, bf16[448,1152]{1,0:T(8,128)(2,1)} %up_hbm.1, bf16[448,1152]{1,0:T(8,128)(2,1)} %bitcast.5), custom_call_target="tpu_custom_call" | custom-call | tf_op jit(solution)/shard_map/pallas_call | solution.py:349
  94.0 0.6 copy.7

commit v4 on v3

--- a/solution.py
+++ b/solution.py
@@ -30,10 +30,15 @@
     ((3, 1), (2, 0), (0, 2), (2, 1)),
     ((1, 2), (3, 2), (2, 3), (2, 2)),
 )
-TURNS = (0, 1, 0, 2, 3, 2, 0, 1, 3, 2, 1, 3, 2, 1, 3, 2, 0, 3, 1, 2, 0, 3, 1, 2, 0, 3, 1, 2, 0, 3, 1, 2, 0, 3, 1, 0)
+TURNS = (
+    0, 1, 0, 1, 12, 2, 0, 13, 1, 14, 4, 15, 6, 2, 3, 6, 7, 5, 4, 6, 7, 5, 3, 6,
+    7, 4, 2, 11, 5, 3, 4, 2, 0, 1, 11, 10, 9, 8, 11, 10, 9, 8, 11, 10, 9, 8, 11, 10,
+    9, 8, 10, 9, 8,
+)
 NQ = len(GROUPS)
 SLOT = {s: i for i, s in enumerate(s for g in GROUPS for s in g)}
 ROWS = HALF * 4
+HROWS = ROWS // 2
 PASS_ON = {
     (0, 0): ((1, 0), (-1, 0), (0, 1), (0, -1)),
     (1, 0): ((0, 1), (0, -1), (1, 0)),
@@ -54,41 +59,38 @@
     return tuple((b, a) for a, b in PASS_ON.get((slot[1], slot[0]), ()))
 
 
-def strip_of(kind, d):
-    return d if kind == 0 else 1 - d
-
-
-def place(kind, hop):
-    return kind * HOPS + hop
+NEAR = ((1, 0), (3, 0), (0, 1), (0, 3))
+TAKEN = (((1, 1), (3, 3), (1, 3)), ((3, 1), (2, 0), (0, 2)), ((2, 1), (1, 2), (3, 2), (2, 3)), ((2, 2),))
+
+
+def length(d, strip):
+    return HOPS if strip == d else HOPS - 1
 
 
 def order():
-    near = ((1, 0), (3, 0), (0, 1), (0, 3))
-    taken = {(0, 0)}
     ops = []
-
-    def take(slots, late):
-        for slot in slots:
-            if slot not in taken:
-                ops.append(("take", slot, late))
-                taken.add(slot)
-
-    at = [0] * NQ
-    for q in TURNS:
-        stage, at[q] = at[q], at[q] + 1
-        if stage == 0:
-            if q == 0:
-                take(near, True)
-                ops += [("pass_on", slot, False) for slot in near]
-            take(GROUPS[q], False)
-            if q == 2:
-                take(GROUPS[3][:3], False)
-            if q == TURNS[0]:
+    at = [0 if turn < 2 else turn % 2 for turn in range(2 * NQ)] + [LAST] * NQ
+    for turn in TURNS:
+        if turn >= 3 * NQ:
+            ops += [("take", slot, (0, 1), None) for slot in TAKEN[turn - 3 * NQ]]
+            continue
+        stage, at[turn] = at[turn], at[turn] + 1
+        if stage == 0 and turn < 2:
+            ops += [("take", slot, (turn,), True) for slot in NEAR]
+            if turn == 0:
                 ops.append(("weights", 0))
-            ops.append(("up", q))
-            continue
-        ops.append(("ring", q, stage))
-        if stage >= LAST:
+            else:
+                ops += [("pass_on", slot, half, False) for half in range(2) for slot in NEAR]
+            ops.append(("up", 0, (turn,)))
+        elif stage == 0:
+            ops.append(("up", turn // 2, (0, 1)))
+        elif turn < 2 * NQ:
+            ops.append(("ring", turn // 2, turn % 2, stage))
+        else:
+            q = turn - 2 * NQ
+            if stage == LAST:
+                ops.append(("finish", q))
+            ops.append(("gather", q, stage - LAST))
             if not any(op[0] == "down" for op in ops):
                 ops.append(("weights", 1))
             ops.append(("down", q, stage - LAST))
@@ -164,43 +166,48 @@
     theirs = swapped[...].astype(F32)
     first = jnp.where(core == 0, mine, theirs)
     second = jnp.where(core == 0, theirs, mine)
-    acts[0:HALF, 0:LOW] = first[:, 0:LOW].astype(BF16)
-    acts[0:HALF, LOW : 2 * LOW] = second[:, 0:LOW].astype(BF16)
-    acts[0:HALF, 2 * LOW : D_CHIP] = (first[:, LOW:PAD] + pltpu.roll(second[:, LOW:PAD], QB, 1)).astype(BF16)
+    tails = (first[:, LOW:PAD] + pltpu.roll(second[:, LOW:PAD], QB, 1)).astype(BF16)
+    for half in range(2):
+        there, here = slice(half * HROWS, half * HROWS + PIECE), slice(half * PIECE, (half + 1) * PIECE)
+        acts[there, 0:LOW] = first[here, 0:LOW].astype(BF16)
+        acts[there, LOW : 2 * LOW] = second[here, 0:LOW].astype(BF16)
+        acts[there, 2 * LOW : D_CHIP] = tails[here]
 
     def acts_rows(slot, half):
-        return acts.at[pl.ds(SLOT[slot] * HALF + half * PIECE, PIECE)]
-
-    def pass_on(slot, urgent):
-        for half in range(2):
-            for sx, sy in steps_of(half, slot):
-                there = ((slot[0] + sx) % NX, (slot[1] + sy) % NY)
-                if urgent is None or (there in GROUPS[1]) == urgent:
+        q, k = SLOT[slot] // 4, SLOT[slot] % 4
+        return acts.at[pl.ds(q * ROWS + half * HROWS + k * PIECE, PIECE)]
+
+    def acts_sem(slot, half):
+        return a_recv.at[NX * NY + NEAR.index(slot) if slot in NEAR and half else SLOT[slot]]
+
+    def pass_on(slot, half, urgent):
+        for sx, sy in steps_of(half, slot):
+            there = ((slot[0] + sx) % NX, (slot[1] + sy) % NY)
+            if urgent is None or (there in GROUPS[1]) == urgent:
+                remote(
+                    acts_rows(slot, half), acts_rows(there, half), acts_sem(there, half), in_plane(sx, sy)
+                ).start()
+
+    for half in range(2):
+        pass_on((0, 0), half, None)
+
+    def take_acts(slot, halves, urgent):
+        arrived(acts.at[pl.ds(0, len(halves) * PIECE)], acts_sem(slot, halves[0]))
+        for half in halves:
+            pass_on(slot, half, urgent)
+
+    def multiply(q, strips):
+        base, rows = strips[0] * HROWS, len(strips) * HROWS
+        for cut in (pl.ds(0, FF), pl.ds(FF, FF)):
+            part[q, base : base + rows, cut] = jnp.dot(
+                acts[q * ROWS + base : q * ROWS + base + rows, :], w[:, cut], preferred_element_type=F32
+            ).astype(BF16)
+            for strip in strips:
+                for d in range(2):
                     remote(
-                        acts_rows(slot, half),
-                        acts_rows(there, half),
-                        a_recv.at[SLOT[there]],
-                        in_plane(sx, sy),
-                    ).start()
-
-    pass_on((0, 0), None)
-
-    def take_acts(slot, late):
-        arrived(acts.at[pl.ds(SLOT[slot] * HALF, HALF)], a_recv.at[SLOT[slot]])
-        pass_on(slot, True if late else None)
-
-    def multiply(q):
-        for cut in (pl.ds(0, FF), pl.ds(FF, FF)):
-            part[q, :, cut] = jnp.dot(
-                acts[q * ROWS : (q + 1) * ROWS, :], w[:, cut], preferred_element_type=F32
-            ).astype(BF16)
-            for kind in range(2):
-                for d in range(2):
-                    at = place(kind, 0)
-                    remote(
-                        rows_of(q, strip_of(kind, d), z_at(d, HOPS - kind)).at[:, cut],
-                        ring.at[q, at, d, :, cut],
-                        r_recv.at[q, at],
+                        rows_of(q, strip, z_at(d, length(d, strip))).at[:, cut],
+                        ring.at[q, strip, 0, d, :, cut],
+                        r_recv.at[q, strip, 0],
                         along_z(toward(d)),
                     ).start()
 
@@ -211,10 +218,11 @@
         return (z + NZ + toward(d) * hops) % NZ
 
     def rows_of(q, strip, owner):
-        return part.at[q, pl.ds(pl.multiple_of(owner * PIECE + strip * STRIP, STRIP), STRIP)]
-
-    def received(q, at):
-        arrived(ring.at[q, at], r_recv.at[q, at])
+        return part.at[q, pl.ds(pl.multiple_of(strip * HROWS + owner * STRIP, STRIP), STRIP)]
+
+    def received(q, strip, hop):
+        ref = ring.at[q, strip, hop] if hop < HOPS - 1 else ring.at[q, strip, hop, strip]
+        arrived(ref, r_recv.at[q, strip, hop])
 
     def piece(owner, q):
         return hidden.at[owner, pl.ds(q * PIECE, PIECE)]
@@ -230,34 +238,27 @@
                     goes = hidden.at[z_at(d, -hop), pl.ds(q * PIECE + d * STRIP, STRIP)]
                 remote(goes, goes, h_recv.at[q, hop], along_z(toward(d))).start()
 
-    def ring_step(q, stage):
-        if stage < LAST:
-            for kind in range(2):
-                left = HOPS - kind - stage
-                if left <= 0:
-                    continue
-                at = place(kind, stage)
-                received(q, at - 1)
-                for d in range(2):
-                    got = ring.at[q, at - 1, d]
-                    own = rows_of(q, strip_of(kind, d), z_at(d, left))
-                    got[...] = (got[...].astype(F32) + own[...].astype(F32)).astype(BF16)
-                    remote(got, ring.at[q, at, d], r_recv.at[q, at], along_z(toward(d))).start()
-            return
-        if stage == LAST:
-            ends = [place(kind, HOPS - kind - 1) for kind in range(2)]
-            for at in ends:
-                received(q, at)
-            for strip in range(2):
-                a, b = ring.at[q, ends[0], strip], ring.at[q, ends[1], 1 - strip]
-                own = rows_of(q, strip, z)
-                gate, up = (
-                    a[:, cut].astype(F32) + b[:, cut].astype(F32) + own[:, cut].astype(F32)
-                    for cut in (pl.ds(0, FF), pl.ds(FF, FF))
-                )
-                value = gate / (1.0 + jnp.exp(-gate)) * up
-                hidden[z, pl.ds(q * PIECE + strip * STRIP, STRIP), :] = value.astype(BF16)
-        gather_step(q, stage - LAST)
+    def ring_step(q, strip, stage):
+        received(q, strip, stage - 1)
+        for d in range(2):
+            left = length(d, strip) - stage
+            if left > 0:
+                got = ring.at[q, strip, stage - 1, d]
+                own = rows_of(q, strip, z_at(d, left))
+                got[...] = (got[...].astype(F32) + own[...].astype(F32)).astype(BF16)
+                remote(got, ring.at[q, strip, stage, d], r_recv.at[q, strip, stage], along_z(toward(d))).start()
+
+    def finish(q):
+        for strip in range(2):
+            received(q, strip, HOPS - 1)
+            a, b = ring.at[q, strip, HOPS - 1, strip], ring.at[q, strip, HOPS - 2, 1 - strip]
+            own = rows_of(q, strip, z)
+            gate, up = (
+                a[:, cut].astype(F32) + b[:, cut].astype(F32) + own[:, cut].astype(F32)
+                for cut in (pl.ds(0, FF), pl.ds(FF, FF))
+            )
+            value = gate / (1.0 + jnp.exp(-gate)) * up
+            hidden[z, pl.ds(q * PIECE + strip * STRIP, STRIP), :] = value.astype(BF16)
 
     def lookup(q, k, axis):
         packed = sum(s[axis] * 4**i for i, s in enumerate(GROUPS[q]))
@@ -319,7 +320,10 @@
         pltpu.make_async_copy(ref, ref, w_local.at[which]).wait()
         arrived(ref, w_recv.at[which])
 
-    act = {"weights": weights, "take": take_acts, "pass_on": pass_on, "up": multiply, "ring": ring_step, "down": down}
+    act = {
+        "weights": weights, "take": take_acts, "pass_on": pass_on, "up": multiply, "ring": ring_step,
+        "finish": finish, "gather": gather_step, "down": down,
+    }
     for name, *at in order():
         act[name](*at)
 
@@ -333,12 +337,13 @@
         value = finals[0, :, cut].astype(F32)
         for k in range(1, NX * NY):
             value = value + finals[k, :, cut].astype(F32)
+        value = jnp.concatenate([value[STRIP * i : STRIP * (i + 1)] for i in (0, 2, 1, 3, 4, 6, 5, 7)], axis=0)
         rows = min(128, D_ROW - tile * 128)
         out_ref[tile * 128 : tile * 128 + rows, :] = value.T[0:rows, :].astype(out_ref.dtype)
 
     for ref in (
-        swapped, w.at[pl.ds(0, D_ROW)], wd.at[0], acts.at[pl.ds(HALF, (NX * NY - 1) * HALF)], ring,
-        hidden.at[pl.ds(0, NZ - 1)], rest, near,
+        swapped, w.at[pl.ds(0, D_ROW)], wd.at[0], acts.at[pl.ds(HALF, (NX * NY - 1) * HALF)],
+        ring.at[pl.ds(0, NQ - 1)], ring.at[NQ - 1, 0], hidden.at[pl.ds(0, NZ - 1)], rest, near,
     ):
         remote(ref, ref, swap_recv, partner).wait_send()
 
@@ -360,7 +365,7 @@
                 pltpu.VMEM((D_CHIP, GU), BF16),
                 pltpu.VMEM((CORES, D_ROW, FF), BF16),
                 pltpu.VMEM((NQ, ROWS, GU), BF16),
-                pltpu.VMEM((NQ, NZ - 1, 2, STRIP, GU), BF16),
+                pltpu.VMEM((NQ, 2, HOPS, 2, STRIP, GU), BF16),
                 pltpu.VMEM((NZ, NQ * PIECE, FF), BF16),
                 pltpu.VMEM((NZ, CORES, NQ * PIECE, PAD), BF16),
                 pltpu.VMEM((NX * NY, TOK, PAD), BF16),
@@ -369,8 +374,8 @@
                 dma((2,)),
                 dma((2,)),
                 dma,
-                dma((NX * NY,)),
-                dma((NQ, NZ - 1)),
+                dma((NX * NY + len(NEAR),)),
+                dma((NQ, 2, HOPS)),
                 dma((NQ, HOPS)),
                 dma((2,)),
             ],

time: 94.7 us -> 92.5 us (0.977)
  Pallas kernels: 94 us -> 91.8 us
    pallas_call x1, Pallas kernels: 94 us -> 91.8 us  [step(): pl.pallas_call(kernel, out_shape=pltpu.VMEM((D_ROW, TOK), BF16), in_specs...]
where the time goes in v4:
time: 92.5 us; the launch traced here: 92.4 us
  Pallas kernels  91.8 us (99%)
    pallas_call x1, Pallas kernels, step(): pl.pallas_call(kernel, out_shape=pltpu.VMEM((D_ROW, TOK), BF16), in_specs...  91.8 us

profile of v4, /device:TPU:1, one launch (start us, length us, event | category | flops | bytes accessed | tf_op | source)
XLA Modules:
  0.0 92.4 jit_solution(7849249577000629832)
XLA Ops:
  0.0 91.8 %shard_map.55 = bf16[448,128]{1,0:T(8,128)(2,1)S(1)} custom-call(s32[448,128]{1,0:T(8,128)} %bitcast.6, f32[7,128]{1,0:T(8,128)} %bitcast.7, bf16[448,1152]{1,0:T(8,128)(2,1)} %gate_hbm.1, bf16[448,1152]{1,0:T(8,128)(2,1)} %up_hbm.1, bf16[448,1152]{1,0:T(8,128)(2,1)} %bitcast.5), custom_call_target="tpu_custom_call" | custom-call | tf_op jit(solution)/shard_map/pallas_call | solution.py:354
  91.8 0.6 copy.7

commit v5 on v4

--- a/solution.py
+++ b/solution.py
@@ -72,11 +72,11 @@
     at = [0 if turn < 2 else turn % 2 for turn in range(2 * NQ)] + [LAST] * NQ
     for turn in TURNS:
         if turn >= 3 * NQ:
-            ops += [("take", slot, (0, 1), None) for slot in TAKEN[turn - 3 * NQ]]
+            ops.append(("take", TAKEN[turn - 3 * NQ], (0, 1), None))
             continue
         stage, at[turn] = at[turn], at[turn] + 1
         if stage == 0 and turn < 2:
-            ops += [("take", slot, (turn,), True) for slot in NEAR]
+            ops += [("take", slots, (turn,), True) for slots in ([(slot,) for slot in NEAR] if turn == 0 else [NEAR])]
             if turn == 0:
                 ops.append(("weights", 0))
             else:
@@ -86,20 +86,20 @@
             ops.append(("up", turn // 2, (0, 1)))
         elif turn < 2 * NQ:
             ops.append(("ring", turn // 2, turn % 2, stage))
+            if turn // 2 == 3 and stage == 1 and ("weights", 1) not in ops:
+                ops.append(("weights", 1))
         else:
             q = turn - 2 * NQ
             if stage == LAST:
                 ops.append(("finish", q))
             ops.append(("gather", q, stage - LAST))
-            if not any(op[0] == "down" for op in ops):
-                ops.append(("weights", 1))
             ops.append(("down", q, stage - LAST))
     return ops
 
 
 def kernel(
     codes_hbm, scales_hbm, gate_hbm, up_hbm, down_hbm, out_ref,
-    codes, scales, staged, swapped, acts, w, wd, part, ring, hidden, outs, finals,
+    codes, scales, staged, swapped, acts, w, wd, part, ring, hidden, outs, finals, sums, wdt,
     sent, in_sem, w_local, w_recv, swap_recv, a_recv, r_recv, h_recv, f_recv,
 ):
     row, col = lax.axis_index("row"), lax.axis_index("col")
@@ -178,7 +178,9 @@
         return acts.at[pl.ds(q * ROWS + half * HROWS + k * PIECE, PIECE)]
 
     def acts_sem(slot, half):
-        return a_recv.at[NX * NY + NEAR.index(slot) if slot in NEAR and half else SLOT[slot]]
+        if slot in NEAR:
+            return a_recv.at[len(NEAR) if half else NEAR.index(slot)]
+        return a_recv.at[len(NEAR) + 1 + next(i for i, slots in enumerate(TAKEN) if slot in slots)]
 
     def pass_on(slot, half, urgent):
         for sx, sy in steps_of(half, slot):
@@ -191,10 +193,11 @@
     for half in range(2):
         pass_on((0, 0), half, None)
 
-    def take_acts(slot, halves, urgent):
-        arrived(acts.at[pl.ds(0, len(halves) * PIECE)], acts_sem(slot, halves[0]))
-        for half in halves:
-            pass_on(slot, half, urgent)
+    def take_acts(slots, halves, urgent):
+        arrived(acts.at[pl.ds(0, len(slots) * len(halves) * PIECE)], acts_sem(slots[0], halves[0]))
+        for slot in slots:
+            for half in halves:
+                pass_on(slot, half, urgent)
 
     def multiply(q, strips):
         base, rows = strips[0] * HROWS, len(strips) * HROWS
@@ -275,9 +278,7 @@
         value = jnp.concatenate([hidden[owner, from_rows, :] for _, owner in turns], axis=0)
 
         def multiply_by(e):
-            product = lax.dot_general(
-                value, wd[e], (((1,), (1,)), ((), ())), preferred_element_type=F32
-            ).astype(BF16)
+            product = jnp.dot(value, wdt[e], preferred_element_type=F32).astype(BF16)
             for i, (turn, _) in enumerate(turns):
                 outs[turn, e, from_rows, 0:D_ROW] = product[i * PIECE : (i + 1) * PIECE]
 
@@ -286,7 +287,7 @@
             to_rows = pl.ds(pl.multiple_of(core * HALF + owner % 2 * PIECE, PIECE), PIECE)
             there = (y + NY - lookup(q, k, 1)) % NY * NX + (x + NX - lookup(q, k, 0)) % NX
 
-            def send(to_core, sem):
+            def send(to_core, sem=1 + q):
                 remote(
                     outs.at[turn, to_core, from_rows],
                     finals.at[q * 4 + k, to_rows],
@@ -302,7 +303,7 @@
             k, to_rows, send = goes_to(turn, owner)
             if q > 0:
                 for e in range(CORES):
-                    send(e, 1)
+                    send(e)
                 continue
 
             @pl.when(k == 0)
@@ -312,13 +313,18 @@
 
             @pl.when(k != 0)
             def _():
-                send(other, 1)
-                send(core, 1)
+                send(other)
+                send(core)
 
     def weights(which):
         ref = w.at[pl.ds(0, D_ROW)] if which == 0 else wd.at[0]
         pltpu.make_async_copy(ref, ref, w_local.at[which]).wait()
         arrived(ref, w_recv.at[which])
+        if which == 1:
+            for e in range(CORES):
+                for tile in range(FF // 128):
+                    cut = slice(tile * 128, (tile + 1) * 128)
+                    wdt[e, cut, :] = wd[e, :, cut].astype(F32).T.astype(BF16)
 
     act = {
         "weights": weights, "take": take_acts, "pass_on": pass_on, "up": multiply, "ring": ring_step,
@@ -329,17 +335,26 @@
 
     rest = finals.at[pl.ds(1, NX * NY - 1)]
     near = finals.at[0, pl.ds(pl.multiple_of(other * HALF, HALF), HALF)]
-    arrived(near, f_recv.at[0])
-    arrived(rest, f_recv.at[1])
-
-    for tile in range(PAD // 128):
-        cut = pl.ds(tile * 128, 128)
-        value = finals[0, :, cut].astype(F32)
-        for k in range(1, NX * NY):
-            value = value + finals[k, :, cut].astype(F32)
-        value = jnp.concatenate([value[STRIP * i : STRIP * (i + 1)] for i in (0, 2, 1, 3, 4, 6, 5, 7)], axis=0)
-        rows = min(128, D_ROW - tile * 128)
-        out_ref[tile * 128 : tile * 128 + rows, :] = value.T[0:rows, :].astype(out_ref.dtype)
+    for q in reversed(range(NQ)):
+        first = 4 * q
+        if q == 0:
+            arrived(near, f_recv.at[0])
+            arrived(finals.at[pl.ds(1, 3)], f_recv.at[1])
+        else:
+            arrived(finals.at[pl.ds(first, 4)], f_recv.at[1 + q])
+        for tile in range(PAD // 128):
+            cut = pl.ds(tile * 128, 128)
+            value = finals[first, :, cut].astype(F32)
+            for k in range(first + 1, first + 4):
+                value = value + finals[k, :, cut].astype(F32)
+            if q < NQ - 1:
+                value = value + sums[:, cut]
+            if q > 0:
+                sums[:, cut] = value
+                continue
+            value = jnp.concatenate([value[STRIP * i : STRIP * (i + 1)] for i in (0, 2, 1, 3, 4, 6, 5, 7)], axis=0)
+            rows = min(128, D_ROW - tile * 128)
+            out_ref[tile * 128 : tile * 128 + rows, :] = value.T[0:rows, :].astype(out_ref.dtype)
 
     for ref in (
         swapped, w.at[pl.ds(0, D_ROW)], wd.at[0], acts.at[pl.ds(HALF, (NX * NY - 1) * HALF)],
@@ -369,15 +384,17 @@
                 pltpu.VMEM((NZ, NQ * PIECE, FF), BF16),
                 pltpu.VMEM((NZ, CORES, NQ * PIECE, PAD), BF16),
                 pltpu.VMEM((NX * NY, TOK, PAD), BF16),
+                pltpu.VMEM((TOK, PAD), F32),
+                pltpu.VMEM((CORES, FF, D_ROW), BF16),
                 dma,
                 dma((2,)),
                 dma((2,)),
                 dma((2,)),
                 dma,
-                dma((NX * NY + len(NEAR),)),
+                dma((len(NEAR) + 1 + len(TAKEN),)),
                 dma((NQ, 2, HOPS)),
                 dma((NQ, HOPS)),
-                dma((2,)),
+                dma((1 + NQ,)),
             ],
             compiler_params=pltpu.CompilerParams(
                 collective_id=0, has_side_effects=True, vmem_limit_bytes=56_000_000

time: 92.5 us -> 92.1 us (level)
  no operation moved by 1% of the time
where the time goes in v5:
time: 92.1 us; the launch traced here: 92 us
  Pallas kernels  91.3 us (99%)
    pallas_call x1, Pallas kernels, step(): pl.pallas_call(kernel, out_shape=pltpu.VMEM((D_ROW, TOK), BF16), in_specs...  91.3 us

profile of v5, /device:TPU:1, one launch (start us, length us, event | category | flops | bytes accessed | tf_op | source)
XLA Modules:
  0.0 92.0 jit_solution(9821877345915169033)
XLA Ops:
  0.0 91.3 %shard_map.55 = bf16[448,128]{1,0:T(8,128)(2,1)S(1)} custom-call(s32[448,128]{1,0:T(8,128)} %bitcast.6, f32[7,128]{1,0:T(8,128)} %bitcast.7, bf16[448,1152]{1,0:T(8,128)(2,1)} %gate_hbm.1, bf16[448,1152]{1,0:T(8,128)(2,1)} %up_hbm.1, bf16[448,1152]{1,0:T(8,128)(2,1)} %bitcast.5), custom_call_target="tpu_custom_call" | custom-call | tf_op jit(solution)/shard_map/pallas_call | solution.py:369
  91.3 0.6 copy.7

commit v6 on v5

--- a/solution.py
+++ b/solution.py
@@ -76,12 +76,14 @@
             continue
         stage, at[turn] = at[turn], at[turn] + 1
         if stage == 0 and turn < 2:
-            ops += [("take", slots, (turn,), True) for slots in ([(slot,) for slot in NEAR] if turn == 0 else [NEAR])]
+            ops += [("take", slots, (turn,), True) for slots in ([(slot,) for slot in NEAR[:3]] if turn == 0 else [NEAR])]
             if turn == 0:
                 ops.append(("weights", 0))
             else:
                 ops += [("pass_on", slot, half, False) for half in range(2) for slot in NEAR]
             ops.append(("up", 0, (turn,)))
+            if turn == 1:
+                ops.append(("take", NEAR[3:], (0,), True))
         elif stage == 0:
             ops.append(("up", turn // 2, (0, 1)))
         elif turn < 2 * NQ:

time: 92.1 us -> 92.1 us (level)
  no operation moved by 1% of the time
where the time goes in v6:
time: 92.1 us; the launch traced here: 92 us
  Pallas kernels  91.3 us (99%)
    pallas_call x1, Pallas kernels, step(): pl.pallas_call(kernel, out_shape=pltpu.VMEM((D_ROW, TOK), BF16), in_specs...  91.3 us

profile of v6, /device:TPU:1, one launch (start us, length us, event | category | flops | bytes accessed | tf_op | source)
XLA Modules:
  0.0 92.0 jit_solution(319019636246796715)
XLA Ops:
  0.0 91.3 %shard_map.55 = bf16[448,128]{1,0:T(8,128)(2,1)S(1)} custom-call(s32[448,128]{1,0:T(8,128)} %bitcast.6, f32[7,128]{1,0:T(8,128)} %bitcast.7, bf16[448,1152]{1,0:T(8,128)(2,1)} %gate_hbm.1, bf16[448,1152]{1,0:T(8,128)(2,1)} %up_hbm.1, bf16[448,1152]{1,0:T(8,128)(2,1)} %bitcast.5), custom_call_target="tpu_custom_call" | custom-call | tf_op jit(solution)/shard_map/pallas_call | solution.py:371
  91.3 0.6 copy.7
